TPU v7x, 32 devices: a whole 2x2x4 slice. The times are simulated.
32 devices in a mesh: ep: 4 (over y, x), fsdp: 8 (over z, core).
Axes of the slice: x: 2, y: 2, z: 4, core: 2. Of those that a mesh axis runs over, the one named last changes fastest.
Arguments:
- master_down: float32 [16, 6400, 4096], P('ep', None, 'fsdp'), may hold values from -0.109375 to 0.109375
- second_down: bfloat16 [16, 6400, 4096], P('ep', None, 'fsdp'), may hold values from -0.0390625 to 0.0390625
- router_weight: float32 [4096, 16], P('fsdp', 'ep'), may hold values from -0.09375 to 0.09375
- router_gain: float32 [4096], P('fsdp'), may hold values from 0.25 to 1.75
Outputs:
- final_down: bfloat16 [16, 6400, 4096], P('ep', 'fsdp')
- scale_down: float32 [16, 6400], P('ep', 'fsdp')
- serve_router: bfloat16 [4096, 16], replicated
All inputs are finite; a program needn't handle non-finite values. Where the computation divides by a largest or mean magnitude, that divisor is 1e-20 or more.
Results may differ from a plain program's by a relative error of at most 0.001.
Values may be sent and summed in bfloat16 or wider, within the bound.
A program may use at most 256 MiB of HBM per device.

v0:
```python
import jax
import jax.numpy as jnp
from jax import lax
from jax.sharding import PartitionSpec as P


def on_device(master_down, second_down, router_weight, router_gain):
    merged_down = master_down + second_down.astype(jnp.float32)
    scale_down = lax.pmax(jnp.max(jnp.abs(merged_down), axis=2), "fsdp")
    narrow_down = (merged_down / jnp.expand_dims(scale_down, 2)).astype(jnp.bfloat16)
    final_down = lax.all_to_all(narrow_down, "fsdp", split_axis=1, concat_axis=2, tiled=True)
    scale_down = lax.dynamic_slice_in_dim(
        scale_down, lax.axis_index("fsdp") * final_down.shape[1], final_down.shape[1], axis=1
    )
    part_router = (router_weight * router_gain[:, None]).astype(jnp.bfloat16)
    row_router = lax.all_gather(part_router, "fsdp", axis=0, tiled=True)
    serve_router = lax.all_gather(row_router, "ep", axis=1, tiled=True)
    return (final_down, scale_down, serve_router)


def solution(mesh):
    placed = (P("ep", None, "fsdp"), P("ep", None, "fsdp"), P("fsdp", "ep"), P("fsdp"))
    return jax.shard_map(
        on_device,
        mesh=mesh,
        in_specs=placed,
        out_specs=(P("ep", "fsdp", None), P("ep", "fsdp"), P()),
        check_vma=False,
    )
```

profile of v0, /device:TPU:0, one launch (start us, length us, event | category | flops | bytes accessed | tf_op | source)
XLA Modules:
  0.0 839.7 jit_solution(15545822426802912631)
XLA Ops:
  7.2 0.0 all-reduce.2.cloned.1.call-start
  7.2 24.2 %abs_reduce_fusion = f32[4,6400]{1,0:T(4,128)S(1)} fusion(f32[4,6400,512]{2,1,0:T(8,128)} %param.4, bf16[4,6400,512]{2,1,0:T(8,128)(2,1)} %param.5), kind=kLoop, calls=%fused_computation.1 | loop fusion | flops 52403200 | bytes 78745600 | tf_op jit(solution)/shard_map/reduce_max | solution.py:9
  31.4 2.3 copy.21
  33.7 0.0 all-reduce.2.cloned.1.call-update
  33.7 82.1 %all-reduce.2.cloned.1.call-done = f32[4,6400]{0,1:T(8,128)} async-done(((f32[4,6400]{0,1:T(8,128)}), f32[4,6400]{0,1:T(8,128)}) %all-reduce.2.cloned.1.call-update) | async-done | bytes 102416 | tf_op jit(solution)/shard_map/pmax | solution.py:9
  115.8 2.4 copy.17
  118.3 34.3 %divide_convert_fusion = bf16[4,6400,512]{2,1,0:T(8,128)(2,1)} fusion(f32[4,6400,512]{2,1,0:T(8,128)} %param.4, bf16[4,6400,512]{2,1,0:T(8,128)(2,1)} %param.5, f32[4,6400]{1,0:T(4,128)S(1)} %copy.17), kind=kLoop, calls=%fused_computation | loop fusion | flops 52428800 | bytes 104960000 | tf_op jit(solution)/shard_map/convert_element_type | solution.py:10
  152.6 33.4 %copy.18 = bf16[4,6400,512]{2,0,1:T(4,128)(2,1)} copy(bf16[4,6400,512]{2,1,0:T(8,128)(2,1)} %divide_convert_fusion) | data formatting | bytes 52428800 | tf_op jit(solution)/shard_map/convert_element_type | solution.py:10
  185.9 0.0 copy-start
  185.9 0.0 copy-start.1
  185.9 6.6 all-to-all-start
  192.6 0.0 copy-done
  192.6 0.0 copy-done.1
  192.6 571.9 %all_gather.6 = bf16[4096,4]{0,1:T(4,128)(2,1)S(1)} all-gather(bf16[512,4]{0,1:T(4,128)(2,1)S(1)} %multiply_convert_fusion), channel_id=1, replica_groups=mesh['ep'=4,'fsdp'=8] {'fsdp'}, dimensions={0}, use_global_device_ids=true | all-gather | bytes 36864 | tf_op jit(solution)/shard_map/all_gather | solution.py:16
  764.5 8.4 %all-gather = bf16[4,4,4096]{2,1,0:T(4,128)(2,1)S(1)} all-gather(bf16[1,4,4096]{2,1,0:T(4,128)(2,1)S(1)} %bitcast.9), channel_id=1, replica_groups=mesh['ep'=4,'fsdp'=8] {'ep'}, dimensions={0}, use_global_device_ids=true | all-gather | bytes 163840 | tf_op jit(solution)/shard_map/all_gather | solution.py:17
  772.9 0.7 reshape.9
  773.6 1.0 constant_dynamic-slice_fusion
  774.6 0.8 copy.20
  775.4 0.0 all-to-all-done
  775.4 18.2 %copy.19 = bf16[4,800,8,512]{3,2,1,0:T(8,128)(2,1)} copy(bf16[4,800,8,512]{3,0,1,2:T(4,128)(2,1)} %bitcast.1) | data formatting | bytes 52428800 | tf_op jit(solution)/shard_map/all_to_all | solution.py:11
  793.7 39.2 %all_to_all.16 = bf16[4,800,4096]{2,1,0:T(8,128)(2,1)} reshape(bf16[4,800,8,512]{3,2,1,0:T(8,128)(2,1)} %copy.19) | data formatting | bytes 52428800 | tf_op jit(solution)/shard_map/all_to_all | solution.py:11
  (1 shorter events, 0.0 us)
Async XLA Ops:
  7.2 108.7 %all-reduce.2.cloned.1.call-start = ((), (), s32[]{:S(2)}) async-start(), calls=%async_computation.1 | async-start | bytes 6553600 | tf_op jit(solution)/shard_map/pmax | solution.py:9
  185.9 6.7 copy-start
  185.9 6.7 copy-start.1
  185.9 589.5 %all-to-all-start = ((bf16[4,6400,512]{2,0,1:T(4,128)(2,1)}), bf16[4,6400,512]{2,0,1:T(4,128)(2,1)}, u32[]{:S(2)}, u32[]{:S(2)}) async-start(bf16[4,6400,512]{2,0,1:T(4,128)(2,1)} %copy.18), calls=%async_computation | async-start | bytes 52428800 | tf_op jit(solution)/shard_map/all_to_all | solution.py:11
Sparse Core Ops, SparseCore 0:
  33.9 81.9 all-reduce.1
where the time goes:
time: 841 us; the launch traced here: 840 us
  blocking collectives  580 us (69%)
  local copies, waits for them, and re-layouts  98 us (12%)
  waiting for transfers between devices  82.1 us (10%)
  other arithmetic  58.5 us (7%)
  between operations  14.1 us (2%)
    all_gather x1, blocking collectives, on_device(): row_router = lax.all_gather(part_router, 'fsdp', axis=0, tiled=True)  572 us
    pmax x1, waiting for transfers between devices, on_device(): scale_down = lax.pmax(jnp.max(jnp.abs(merged_down), axis=2), 'fsdp')  82.1 us
    all_to_all x2, local copies, waits for them, and re-layouts, on_device(): lax.all_to_all(narrow_down, 'fsdp', split_axis=1, concat_axis=2, tiled=True)  57.4 us
    convert_element_type x1, other arithmetic, on_device(): (merged_down / jnp.expand_dims(scale_down, 2)).astype(jnp.bfloat16)  34.3 us
    convert_element_type x1, local copies, waits for them, and re-layouts, on_device(): (merged_down / jnp.expand_dims(scale_down, 2)).astype(jnp.bfloat16)  33.4 us
    reduce_max x1, other arithmetic, on_device(): scale_down = lax.pmax(jnp.max(jnp.abs(merged_down), axis=2), 'fsdp')  24.2 us
  transfers between devices with their start and end apart: 2, of which 1 were waited for; matrix products, arithmetic and copies ran while one was open for 0% of the time, Pallas kernels for 0%

commit v1 on v0

--- a/solution.py
+++ b/solution.py
@@ -1,14 +1,25 @@
+import functools
 import jax
 import jax.numpy as jnp
 from jax import lax
 from jax.sharding import PartitionSpec as P
 
 
+def works_cut(payload, axis_k, join_dim):
+    raw_out = lax.axis_size("fsdp")
+    m_next = jnp.split(payload, raw_out, axis=axis_k)
+    f_now = lax.all_to_all(jnp.stack(m_next), "fsdp", split_axis=0, concat_axis=0)
+    return jnp.concatenate(f_now, axis=join_dim)
+
+
+paths_open = functools.partial(works_cut, axis_k=1, join_dim=2)
+
+
 def on_device(master_down, second_down, router_weight, router_gain):
     merged_down = master_down + second_down.astype(jnp.float32)
     scale_down = lax.pmax(jnp.max(jnp.abs(merged_down), axis=2), "fsdp")
     narrow_down = (merged_down / jnp.expand_dims(scale_down, 2)).astype(jnp.bfloat16)
-    final_down = lax.all_to_all(narrow_down, "fsdp", split_axis=1, concat_axis=2, tiled=True)
+    final_down = paths_open(narrow_down)
     scale_down = lax.dynamic_slice_in_dim(
         scale_down, lax.axis_index("fsdp") * final_down.shape[1], final_down.shape[1], axis=1
     )

time: 841 us -> 767 us (0.912)
  local copies, waits for them, and re-layouts: 98 us -> 50.6 us
  waiting for transfers between devices: 82.1 us -> 55.3 us
    all_to_all x2 -> x0, local copies, waits for them, and re-layouts: 57.4 us -> none  [on_device(): lax.all_to_all(narrow_down, 'fsdp', split_axis=1, concat_axis=2, tiled=True)]
    convert_element_type x1 -> x0, local copies, waits for them, and re-layouts: 33.4 us -> none  [on_device(): (merged_down / jnp.expand_dims(scale_down, 2)).astype(jnp.bfloat16)]
    pmax x1, waiting for transfers between devices: 82.1 us -> 55.3 us  [on_device(): scale_down = lax.pmax(jnp.max(jnp.abs(merged_down), axis=2), 'fsdp')]
    unnamed x7 -> x12, local copies, waits for them, and re-layouts: 3.75 us -> 27.5 us
    reshape x0 -> x1, local copies, waits for them, and re-layouts: none -> 17.9 us  [works_cut(): return jnp.concatenate(f_now, axis=join_dim)]
where the time goes in v1:
time: 767 us; the launch traced here: 766 us
  blocking collectives  580 us (76%)
  other arithmetic  59.2 us (8%)
  waiting for transfers between devices  55.3 us (7%)
  local copies, waits for them, and re-layouts  50.6 us (7%)
  between operations  14.1 us (2%)
    all_gather x1, blocking collectives, on_device(): row_router = lax.all_gather(part_router, 'fsdp', axis=0, tiled=True)  572 us
    pmax x1, waiting for transfers between devices, on_device(): scale_down = lax.pmax(jnp.max(jnp.abs(merged_down), axis=2), 'fsdp')  55.3 us
    convert_element_type x1, other arithmetic, on_device(): (merged_down / jnp.expand_dims(scale_down, 2)).astype(jnp.bfloat16)  34.4 us
    unnamed x12, local copies, waits for them, and re-layouts  27.5 us
    reduce_max x1, other arithmetic, on_device(): scale_down = lax.pmax(jnp.max(jnp.abs(merged_down), axis=2), 'fsdp')  24.9 us
    reshape x1, local copies, waits for them, and re-layouts, works_cut(): return jnp.concatenate(f_now, axis=join_dim)  17.9 us
  transfers between devices with their start and end apart: 2, of which 1 were waited for; matrix products, arithmetic and copies ran while one was open for 0% of the time, Pallas kernels for 0%

profile of v1, /device:TPU:0, one launch (start us, length us, event | category | flops | bytes accessed | tf_op | source)
XLA Modules:
  0.0 766.2 jit_solution(10804507981940321855)
XLA Ops:
  7.2 0.0 all-reduce.2.cloned.1.call-start
  7.2 24.9 %abs_reduce_fusion = f32[4,6400]{1,0:T(4,128)} fusion(f32[4,6400,512]{2,1,0:T(8,128)} %param.4, bf16[4,6400,512]{2,1,0:T(8,128)(2,1)} %param.5), kind=kLoop, calls=%fused_computation.1 | loop fusion | flops 52403200 | bytes 78745600 | tf_op jit(solution)/shard_map/reduce_max | solution.py:20
  32.1 0.0 all-reduce.2.cloned.1.call-update
  32.1 55.3 %all-reduce.2.cloned.1.call-done = f32[4,6400]{1,0:T(4,128)} async-done(((f32[4,6400]{1,0:T(4,128)}), f32[4,6400]{1,0:T(4,128)}) %all-reduce.2.cloned.1.call-update) | async-done | bytes 102416 | tf_op jit(solution)/shard_map/pmax | solution.py:20
  87.4 34.4 %divide_convert_fusion = bf16[4,6400,512]{2,1,0:T(8,128)(2,1)} fusion(f32[4,6400,512]{2,1,0:T(8,128)} %param.4, bf16[4,6400,512]{2,1,0:T(8,128)(2,1)} %param.5, f32[4,6400]{1,0:T(4,128)} %all-reduce.2.cloned.1.call-done), kind=kLoop, calls=%fused_computation | loop fusion | flops 52428800 | bytes 104960000 | tf_op jit(solution)/shard_map/convert_element_type | solution.py:21
  121.8 3.8 fusion.7
  125.6 3.8 fusion.6
  129.5 3.8 fusion.5
  133.2 3.8 fusion.4
  137.1 3.9 fusion.3
  141.0 3.8 fusion.2
  144.8 3.8 fusion.1
  148.6 3.8 fusion
  152.4 0.0 copy-start
  152.4 0.0 copy-start.1
  152.4 6.6 all-to-all-start
  159.1 0.0 copy-done
  159.1 0.0 copy-done.1
  159.1 571.9 %all_gather.6 = bf16[4096,4]{0,1:T(4,128)(2,1)S(1)} all-gather(bf16[512,4]{0,1:T(4,128)(2,1)S(1)} %multiply_convert_fusion), channel_id=1, replica_groups=mesh['ep'=4,'fsdp'=8] {'fsdp'}, dimensions={0}, use_global_device_ids=true | all-gather | bytes 36864 | tf_op jit(solution)/shard_map/all_gather | solution.py:27
  731.0 8.4 %all-gather = bf16[4,4,4096]{2,1,0:T(4,128)(2,1)S(1)} all-gather(bf16[1,4,4096]{2,1,0:T(4,128)(2,1)S(1)} %bitcast.40), channel_id=1, replica_groups=mesh['ep'=4,'fsdp'=8] {'ep'}, dimensions={0}, use_global_device_ids=true | all-gather | bytes 163840 | tf_op jit(solution)/shard_map/all_gather | solution.py:28
  739.4 0.7 reshape.17
  740.1 1.4 constant_dynamic-slice_fusion
  741.5 0.0 all-to-all-done
  741.5 17.9 %copy.9 = bf16[8,4,100,8,512]{4,3,0,2,1:T(8,128)(2,1)} copy(bf16[8,4,100,8,512]{4,3,2,1,0:T(8,128)(2,1)} %bitcast.13) | data formatting | bytes 52428800 | tf_op jit(solution)/shard_map/reshape | solution.py:12
  (1 shorter events, 0.0 us)
Async XLA Ops:
  7.2 80.3 %all-reduce.2.cloned.1.call-start = ((), (), s32[]{:S(2)}) async-start(), calls=%async_computation.1 | async-start | bytes 204800 | tf_op jit(solution)/shard_map/pmax | solution.py:20
  152.4 6.6 copy-start
  152.4 6.6 copy-start.1
  152.4 589.1 %all-to-all-start = ((bf16[8,4,800,512]{3,2,1,0:T(8,128)(2,1)}), bf16[8,4,800,512]{3,2,1,0:T(8,128)(2,1)}, u32[]{:S(2)}, u32[]{:S(2)}) async-start(bf16[8,4,800,512]{3,2,1,0:T(8,128)(2,1)} %fusion), calls=%async_computation | async-start | bytes 52428800 | tf_op jit(solution)/shard_map/all_to_all | solution.py:11
Sparse Core Ops, SparseCore 0:
  32.2 55.1 all-reduce.1
